TPU v7x, 16 devices: a whole 2x2x2 slice. The times are simulated.
16 devices in a mesh: data: 16 (over z, y, x, core).
Axes of the slice: x: 2, y: 2, z: 2, core: 2. Of those that a mesh axis runs over, the one named last changes fastest.
Arguments:
- feat_a: bfloat16 [2048, 512], P('data')
- feat_b: bfloat16 [2048, 512], P('data')
- w_one: bfloat16 [512, 2048], replicated
- w_two: bfloat16 [2048, 2048], replicated
- w_three: bfloat16 [2048, 2048], replicated
- g_one: float32 [2048], replicated
- b_one: float32 [2048], replicated
- g_two: float32 [2048], replicated
- b_two: float32 [2048], replicated
- lam_off: float32 [], replicated
Outputs:
- output 1: float32 [], replicated
- output 2: float32 [512, 2048], replicated
- output 3: float32 [2048, 2048], replicated
- output 4: float32 [2048, 2048], replicated
- output 5: float32 [2048], replicated
- output 6: float32 [2048], replicated
- output 7: float32 [2048], replicated
- output 8: float32 [2048], replicated
All inputs are finite; a program needn't handle non-finite values.
Results may differ from a plain program's by a relative error of at most 0.00475.
Values are sent between devices in bfloat16 or wider.
A program may use at most 1 GiB of HBM per device.

v0:
```python
import jax
import jax.numpy as jnp
from jax import lax
from jax.sharding import PartitionSpec as P

NORM_EPS = 1e-5
BATCH_AXIS = 'data'


def global_norm(pre, rows_all):
    stat_sums = lax.psum(jnp.stack([jnp.sum(pre, axis=1), jnp.sum(pre * pre, axis=1)]), BATCH_AXIS)
    mean_val = stat_sums[0] / rows_all
    var_val = stat_sums[1] / rows_all - mean_val * mean_val
    inv_std = lax.rsqrt(var_val + NORM_EPS)[:, None, :]
    return (pre - mean_val[:, None, :]) * inv_std, inv_std


def global_norm_back(grad_norm, normed, inv_std, rows_all):
    stat_sums = lax.psum(jnp.stack([jnp.sum(grad_norm, axis=1), jnp.sum(grad_norm * normed, axis=1)]), BATCH_AXIS)
    mean_grad = (stat_sums[0] / rows_all)[:, None, :]
    mean_cross = (stat_sums[1] / rows_all)[:, None, :]
    return inv_std * (grad_norm - mean_grad - normed * mean_cross)


def corr_loss(corr, lam_off, width):
    diag_c = jnp.diagonal(corr)
    loss_val = jnp.sum((1.0 - diag_c) ** 2) + lam_off * (jnp.sum(corr * corr) - jnp.sum(diag_c * diag_c))
    on_diag = jnp.arange(width)[:, None] == jnp.arange(width)[None, :]
    grad_c = jnp.where(on_diag, -2.0 * (1.0 - corr), 2.0 * lam_off * corr).astype(jnp.bfloat16)
    return loss_val, grad_c


def solution(mesh):
    num_devs = mesh.shape[BATCH_AXIS]

    def local_step(feat_a, feat_b, w_one, w_two, w_three, g_one, b_one, g_two, b_two, lam_off):
        rows_all = feat_a.shape[0] * num_devs
        width = w_two.shape[0]
        features = jnp.stack([feat_a, feat_b])
        pre_one = jnp.einsum('vnf,fd->vnd', features, w_one, preferred_element_type=jnp.float32)
        norm_one, inv_one = global_norm(pre_one, rows_all)
        aff_one = norm_one * g_one + b_one
        act_one = jnp.maximum(aff_one, 0.0).astype(jnp.bfloat16)
        pre_two = jnp.einsum('woe,ef->wof', act_one, w_two, preferred_element_type=jnp.float32)
        norm_two, inv_two = global_norm(pre_two, rows_all)
        aff_two = norm_two * g_two + b_two
        act_two = jnp.maximum(aff_two, 0.0).astype(jnp.bfloat16)
        proj_out = jnp.einsum('woe,ef->wof', act_two, w_three, preferred_element_type=jnp.float32)
        norm_out, inv_out = global_norm(proj_out, rows_all)
        emb = norm_out.astype(jnp.bfloat16)
        part_corr = jnp.einsum('nd,ne->de', emb[0], emb[1], preferred_element_type=jnp.float32)
        corr = lax.psum(part_corr, BATCH_AXIS) / rows_all
        loss_val, grad_c = corr_loss(corr, lam_off, width)
        grad_a = jnp.einsum('ne,de->nd', emb[1], grad_c, preferred_element_type=jnp.float32)
        grad_b = jnp.einsum('nd,de->ne', emb[0], grad_c, preferred_element_type=jnp.float32)
        grad_emb = jnp.stack([grad_a, grad_b]) / rows_all
        grad_proj = global_norm_back(grad_emb, norm_out, inv_out, rows_all).astype(jnp.bfloat16)
        dw_three = jnp.einsum('woe,wof->ef', act_two, grad_proj, preferred_element_type=jnp.float32)
        grad_act_two = jnp.einsum('wof,ef->woe', grad_proj, w_three, preferred_element_type=jnp.float32)
        grad_aff_two = jnp.where(aff_two > 0, grad_act_two, 0.0)
        dg_two = jnp.sum(grad_aff_two * norm_two, axis=(0, 1))
        db_two = jnp.sum(grad_aff_two, axis=(0, 1))
        grad_pre_two = global_norm_back(grad_aff_two * g_two, norm_two, inv_two, rows_all).astype(jnp.bfloat16)
        dw_two = jnp.einsum('woe,wof->ef', act_one, grad_pre_two, preferred_element_type=jnp.float32)
        grad_act_one = jnp.einsum('wof,ef->woe', grad_pre_two, w_two, preferred_element_type=jnp.float32)
        grad_aff_one = jnp.where(aff_one > 0, grad_act_one, 0.0)
        dg_one = jnp.sum(grad_aff_one * norm_one, axis=(0, 1))
        db_one = jnp.sum(grad_aff_one, axis=(0, 1))
        grad_pre_one = global_norm_back(grad_aff_one * g_one, norm_one, inv_one, rows_all).astype(jnp.bfloat16)
        dw_one = jnp.einsum('vnf,vnd->fd', features, grad_pre_one, preferred_element_type=jnp.float32)
        totals = lax.psum((dw_one, dw_two, dw_three, dg_one, db_one, dg_two, db_two), BATCH_AXIS)
        return (loss_val,) + tuple(totals)

    row_spec = P(BATCH_AXIS, None)
    return jax.shard_map(local_step, mesh=mesh, in_specs=(row_spec, row_spec, P(), P(), P(), P(), P(), P(), P(), P()), out_specs=(P(), P(), P(), P(), P(), P(), P(), P()), check_vma=False)
```

profile of v0, /device:TPU:0, one launch (start us, length us, event | category | flops | bytes accessed | tf_op | source)
XLA Modules:
  0.0 885.7 jit_solution(15045098465455738623)
XLA Ops:
  7.2 1.5 copy-done
  8.8 3.1 fusion.49
  11.9 34.8 %psum.98 = f32[2,2,2048]{2,1,0:T(2,128)S(1)} all-reduce(f32[2,2,2048]{2,1,0:T(2,128)S(1)} %pad_maximum_fusion.3), channel_id=1, replica_groups=mesh['data'=16] {'data'}, use_global_device_ids=true, to_apply=%region_2.0 | all-reduce | flops 8192 | bytes 65536 | tf_op jit(solution)/shard_map/psum | solution.py:11
  46.8 7.7 fusion.48
  54.6 32.8 %psum.99 = f32[2,2,2048]{2,1,0:T(2,128)S(1)} all-reduce(f32[2,2,2048]{2,1,0:T(2,128)S(1)} %pad_maximum_fusion.4), channel_id=1, replica_groups=mesh['data'=16] {'data'}, use_global_device_ids=true, to_apply=%region_5.0 | all-reduce | flops 8192 | bytes 65536 | tf_op jit(solution)/shard_map/psum | solution.py:11
  87.5 6.4 fusion.47
  93.9 32.8 %psum.100 = f32[2,2,2048]{2,1,0:T(2,128)S(1)} all-reduce(f32[2,2,2048]{2,1,0:T(2,128)S(1)} %pad_maximum_fusion.5), channel_id=1, replica_groups=mesh['data'=16] {'data'}, use_global_device_ids=true, to_apply=%region_8.0 | all-reduce | flops 8192 | bytes 65536 | tf_op jit(solution)/shard_map/psum | solution.py:11
  127.0 8.5 fusion.23
  136.5 180.0 %all-reduce.6.cloned.1.call-done = f32[2048,2048]{1,0:T(8,128)} async-done(((f32[2048,2048]{1,0:T(8,128)}), f32[2048,2048]{1,0:T(8,128)}) %all-reduce.6.cloned.1.call-update) | async-done | bytes 16777232 | tf_op jit(solution)/shard_map/psum | solution.py:52
  316.4 9.7 %convolution_bitcast_fusion.4 = f32[1,128,2048]{2,1,0:T(8,128)} fusion(bf16[2,128,2048]{2,1,0:T(8,128)(2,1)S(1)} %fusion.16, f32[2048,2048]{1,0:T(8,128)} %all-reduce.6.cloned.1.call-done, f32[]{:T(128)S(6)} %mul.183), kind=kOutput, calls=%fused_computation.19 | convolution fusion | flops 1103101952 | bytes 18350084 | tf_op jit(solution)/shard_map/ne,de->nd/dot_general | solution.py:54
  326.1 1.2 copy-done.3
  327.4 1.7 convolution_bitcast_fusion.3
  330.0 31.6 %psum.102 = f32[2,2,2048]{2,1,0:T(2,128)S(1)} all-reduce(f32[2,2,2048]{2,1,0:T(2,128)S(1)} %pad_maximum_fusion.6), channel_id=1, replica_groups=mesh['data'=16] {'data'}, use_global_device_ids=true, to_apply=%region_15.16 | all-reduce | flops 8192 | bytes 65536 | tf_op jit(solution)/shard_map/psum | solution.py:19
  361.6 2.2 multiply_convert_fusion.2
  363.9 8.3 multiply_reduce_fusion.1
  372.2 33.1 %psum.103 = f32[2,2,2048]{2,1,0:T(2,128)S(1)} all-reduce(f32[2,2,2048]{2,1,0:T(2,128)S(1)} %pad_maximum_fusion.7), channel_id=1, replica_groups=mesh['data'=16] {'data'}, use_global_device_ids=true, to_apply=%region_18.19 | all-reduce | flops 8192 | bytes 65536 | tf_op jit(solution)/shard_map/psum | solution.py:19
  405.3 2.9 multiply_convert_fusion.1
  408.2 8.4 multiply_reduce_fusion.2
  416.6 8.6 convolution_bitcast_fusion.1
  425.2 0.6 pad_maximum_fusion.8
  426.2 9.7 %convolution_bitcast_fusion = f32[2048,2048]{1,0:T(8,128)} fusion(bf16[2,128,2048]{2,1,0:T(8,128)(2,1)S(1)} %multiply_convert_fusion.2, f32[2,128,2048]{2,1,0:T(8,128)} %get-tuple-element.43, f32[2048]{0:T(1024)S(1)} %copy-done.12, f32[2048]{0:T(1024)S(1)} %copy-done.9, f32[2,2048]{1,0:T(2,128)S(1)} %fusion.38, f32[2,2048]{1,0:T(2,128)S(1)} %fusion.39), kind=kOutput, calls=%fused_computation.4 | convolution fusion | flops 2150629376 | bytes 19972096 | tf_op jit(solution)/shard_map/woe,wof->ef/dot_general | solution.py:58
  435.9 58.1 %all-reduce.8.cloned.1.call-done = (f32[2,2,2048]{2,1,0:T(2,128)}, f32[2048]{0:T(1024)}, f32[2048]{0:T(1024)}, f32[2048]{0:T(1024)}, f32[2048]{0:T(1024)}) async-done(((f32[2,2,2048]{2,1,0:T(2,128)}, f32[2048]{0:T(1024)}, f32[2048]{0:T(1024)}, f32[2048]{0:T(1024)}, f32[2048]{0:T(1024)}), (f32[2,2,2048]{2,1,0:T(2,128)}, f32[2048]{0:T(1024)}, f32[2048]{0:T(1024)}, f32[2048]{0:T(1024)}, ...) | async-done | bytes 65552 | tf_op jit(solution)/shard_map/psum | solution.py:19
  494.0 0.8 fusion.25
  494.7 4.5 convolution_bitcast_fusion.2
  499.3 13.5 %multiply_reduce_fusion = (f32[]{:T(128)}, f32[2048,2048]{1,0:T(8,128)}) fusion(f32[2048,2048]{1,0:T(8,128)} %all-reduce.6.cloned.1.call-done), kind=kLoop, calls=%fused_computation.3 | loop fusion | flops 12582911 | bytes 33554436 | tf_op jit(solution)/shard_map/reduce_sum | solution.py:27
  512.7 34.0 %gather_fusion = f32[2048]{0:T(1024)S(1)} fusion(f32[2048,2048]{1,0:T(8,128)} %get-tuple-element.35, s32[2048]{0:T(1024)S(1)} %bitcast.112), kind=kCustom, calls=%fused_computation | custom fusion | bytes 32768 | tf_op jit(solution)/shard_map/jit(diagonal)/cond/branch_0_fun/gather | solution.py:26
  546.8 0.6 multiply_reduce_fusion.11
  549.3 299.7 %all-reduce.10.cloned.1.call-done = (f32[512,2048]{1,0:T(8,128)}, f32[2048,2048]{1,0:T(8,128)}, f32[2048,2048]{1,0:T(8,128)}) async-done(((f32[512,2048]{1,0:T(8,128)}, f32[2048,2048]{1,0:T(8,128)}, f32[2048,2048]{1,0:T(8,128)}), (f32[512,2048]{1,0:T(8,128)}, f32[2048,2048]{1,0:T(8,128)}, f32[2048,2048]{1,0:T(8,128)})) %all-reduce.10.cloned.1.call-update) | async-done | bytes 37748752 | tf_op jit(solution)/shard_map/psum | solution.py:71
  849.1 4.8 copy.37
  853.9 13.6 %copy.38 = f32[2048,2048]{1,0:T(8,128)} copy(f32[2048,2048]{1,0:T(8,128)} %get-tuple-element.49) | data formatting | bytes 33554432
  867.5 1.7 slice-done.3
  869.2 6.3 copy.39
  (66 shorter events, 4.5 us)
Async XLA Ops:
  7.2 1.6 copy-start
  7.2 309.3 %all-reduce.6.cloned.1.call-start = ((), (), s32[]{:S(2)}) async-start(), calls=%async_computation | async-start | bytes 33554432 | tf_op jit(solution)/shard_map/psum | solution.py:52
  8.8 38.0 %copy-start.10 = (f32[2048]{0:T(1024)S(1)}, f32[2048]{0:T(1024)}, u32[]{:S(2)}) copy-start(f32[2048]{0:T(1024)} %param.15) | copy-start | bytes 24580
  8.8 38.0 %copy-start.11 = (f32[2048]{0:T(1024)S(1)}, f32[2048]{0:T(1024)}, u32[]{:S(2)}) copy-start(f32[2048]{0:T(1024)} %param.16) | copy-start | bytes 24580
  46.8 40.7 %copy-start.9 = (f32[2048]{0:T(1024)S(1)}, f32[2048]{0:T(1024)}, u32[]{:S(2)}) copy-start(f32[2048]{0:T(1024)} %param.17) | copy-start | bytes 24580
  46.8 40.7 %copy-start.12 = (f32[2048]{0:T(1024)S(1)}, f32[2048]{0:T(1024)}, u32[]{:S(2)}) copy-start(f32[2048]{0:T(1024)} %param.18) | copy-start | bytes 24580
  135.6 358.4 %all-reduce.8.cloned.1.call-start = ((), (), s32[]{:S(2)}) async-start(), calls=%async_computation.1 | async-start | bytes 131072 | tf_op jit(solution)/shard_map/psum | solution.py:19
  316.4 10.9 %copy-start.3 = (f32[2048,2048]{1,0:T(8,128)S(1)}, f32[2048,2048]{1,0:T(8,128)}, u32[]{:S(2)}) copy-start(f32[2048,2048]{1,0:T(8,128)} %all-reduce.6.cloned.1.call-done) | copy-start | bytes 50331652
  327.4 1.7 copy-start.5
  329.0 1.0 copy-start.6
  361.6 2.2 copy-start.4
  405.3 2.9 copy-start.2
  425.8 68.9 %copy-start.7 = (bf16[128,512]{1,0:T(8,128)(2,1)S(1)}, bf16[128,512]{1,0:T(8,128)(2,1)}, u32[]{:S(2)}) copy-start(bf16[128,512]{1,0:T(8,128)(2,1)} %param.11) | copy-start | bytes 393220
  425.8 68.9 %copy-start.8 = (bf16[128,512]{1,0:T(8,128)(2,1)S(1)}, bf16[128,512]{1,0:T(8,128)(2,1)}, u32[]{:S(2)}) copy-start(bf16[128,512]{1,0:T(8,128)(2,1)} %param.10) | copy-start | bytes 393220
  425.9 423.2 %all-reduce.10.cloned.1.call-start = ((), (), s32[]{:S(2)}) async-start(), calls=%async_computation.2 | async-start | bytes 75497472 | tf_op jit(solution)/shard_map/psum | solution.py:71
  849.1 18.4 %slice-start = ((s8[16777216]{0:T(1024)(128)(4,1)}), s8[4194304]{0:T(1024)(128)(4,1)S(1)}, s32[]{:S(2)}) async-start(s8[16777216]{0:T(1024)(128)(4,1)} %bitcast.113), calls=%async_computation.3 | async-start | bytes 8388608
  853.9 13.6 %slice-start.1 = ((s8[16777216]{0:T(1024)(128)(4,1)}), s8[4194304]{0:T(1024)(128)(4,1)S(1)}, s32[]{:S(2)}) async-start(s8[16777216]{0:T(1024)(128)(4,1)} %bitcast.113), calls=%async_computation.4 | async-start | bytes 8388608
  853.9 13.6 %slice-start.2 = ((s8[16777216]{0:T(1024)(128)(4,1)}), s8[4194304]{0:T(1024)(128)(4,1)S(1)}, s32[]{:S(2)}) async-start(s8[16777216]{0:T(1024)(128)(4,1)} %bitcast.113), calls=%async_computation.5 | async-start | bytes 8388608
  853.9 15.3 %slice-start.3 = ((s8[16777216]{0:T(1024)(128)(4,1)}), s8[4194304]{0:T(1024)(128)(4,1)S(1)}, s32[]{:S(2)}) async-start(s8[16777216]{0:T(1024)(128)(4,1)} %bitcast.113), calls=%async_computation.6 | async-start | bytes 8388608
  869.2 6.4 copy-start.16
  869.2 7.0 copy-start.15
  869.2 7.6 copy-start.14
  869.2 8.2 copy-start.13
  869.2 8.8 copy-start.1
Sparse Core Ops, SparseCore 0:
  135.7 180.6 all-reduce.5
  426.0 67.9 all-reduce.7
  501.0 348.0 all-reduce.9
where the time goes:
time: 888 us; the launch traced here: 886 us
  waiting for transfers between devices  538 us (61%)
  blocking collectives  165 us (19%)
  matrix products  76.6 us (9%)
  local copies, waits for them, and re-layouts  66.2 us (7%)
  other arithmetic  21.6 us (2%)
  between operations  17.8 us (2%)
    psum x1, waiting for transfers between devices, local_step(): lax.psum((dw_one, dw_two, dw_three, dg_one, db_one, dg_two, db_two), BATC...  300 us
    psum x1, waiting for transfers between devices, local_step(): corr = lax.psum(part_corr, BATCH_AXIS) / rows_all  180 us
    psum x3, blocking collectives, global_norm(): lax.psum(jnp.stack([jnp.sum(pre, axis=1), jnp.sum(pre * pre, axis=1)]), B...  101 us
    psum x2, blocking collectives, global_norm_back(): lax.psum(jnp.stack([jnp.sum(grad_norm, axis=1), jnp.sum(grad_norm * norme...  64.6 us
    psum x1, waiting for transfers between devices, global_norm_back(): lax.psum(jnp.stack([jnp.sum(grad_norm, axis=1), jnp.sum(grad_norm * norme...  58.1 us
    gather x1, local copies, waits for them, and re-layouts, corr_loss(): diag_c = jnp.diagonal(corr)  34 us
    unnamed x49, local copies, waits for them, and re-layouts  32.1 us
  transfers between devices with their start and end apart: 3, of which 3 were waited for; matrix products, arithmetic and copies ran while one was open for 7% of the time, Pallas kernels for 0%

commit v1 on v0

v1 whole, which is shorter than its diff:
```python
import jax
import jax.numpy as jnp
from jax import lax
from jax.sharding import PartitionSpec as P

NORM_EPS = 1e-5
BATCH_AXIS = 'data'


def normalize(pre):
    mean_val = jnp.mean(pre, axis=0)
    var_val = jnp.mean(pre * pre, axis=0) - mean_val * mean_val
    inv_std = lax.rsqrt(var_val + NORM_EPS)
    return (pre - mean_val) * inv_std, inv_std


def normalize_back(grad_norm, normed, inv_std):
    centred = grad_norm - jnp.mean(grad_norm, axis=0)
    return inv_std * (centred - normed * jnp.mean(grad_norm * normed, axis=0))


def mm(a, b, ca, cb):
    return lax.dot_general(a, b, (((ca,), (cb,)), ((), ())), preferred_element_type=jnp.float32)


def solution(mesh):
    num_devs = mesh.shape[BATCH_AXIS]
    pairs = [(d, d ^ 1) for d in range(num_devs)]

    def swap(value):
        return lax.ppermute(value, BATCH_AXIS, pairs)

    def local_step(feat_a, feat_b, w_one, w_two, w_three, g_one, b_one, g_two, b_two, lam_off):
        rows_all = feat_a.shape[0] * num_devs
        width = w_two.shape[0]
        view = lax.axis_index(BATCH_AXIS) % 2
        both = lax.all_gather(jnp.stack([feat_a, feat_b]), BATCH_AXIS)
        feat = lax.dynamic_index_in_dim(both, view, 1, keepdims=False).reshape(rows_all, -1)
        norm_one, inv_one = normalize(mm(feat, w_one, 1, 0))
        aff_one = norm_one * g_one + b_one
        act_one = jnp.maximum(aff_one, 0.0).astype(jnp.bfloat16)
        norm_two, inv_two = normalize(mm(act_one, w_two, 1, 0))
        aff_two = norm_two * g_two + b_two
        act_two = jnp.maximum(aff_two, 0.0).astype(jnp.bfloat16)
        norm_out, inv_out = normalize(mm(act_two, w_three, 1, 0))
        emb = norm_out.astype(jnp.bfloat16)
        other = swap(emb)
        corr = mm(emb, other, 0, 0) / rows_all
        on_diag = jnp.arange(width)[:, None] == jnp.arange(width)[None, :]
        loss_own = jnp.sum(jnp.where(on_diag, (1.0 - corr) ** 2, lam_off * corr * corr))
        loss_val = jnp.where(view == 0, loss_own, swap(loss_own))
        grad_c = jnp.where(on_diag, -2.0 * (1.0 - corr), 2.0 * lam_off * corr).astype(jnp.bfloat16)
        grad_emb = mm(other, grad_c, 1, 1) / rows_all
        grad_proj = normalize_back(grad_emb, norm_out, inv_out).astype(jnp.bfloat16)
        dw_three = mm(act_two, grad_proj, 0, 0)
        dw_three = dw_three + swap(dw_three)
        grad_aff_two = jnp.where(aff_two > 0, mm(grad_proj, w_three, 1, 1), 0.0)
        dg_two = jnp.sum(grad_aff_two * norm_two, axis=0)
        db_two = jnp.sum(grad_aff_two, axis=0)
        grad_pre_two = normalize_back(grad_aff_two * g_two, norm_two, inv_two).astype(jnp.bfloat16)
        dw_two = mm(act_one, grad_pre_two, 0, 0)
        dw_two = dw_two + swap(dw_two)
        grad_aff_one = jnp.where(aff_one > 0, mm(grad_pre_two, w_two, 1, 1), 0.0)
        dg_one = jnp.sum(grad_aff_one * norm_one, axis=0)
        db_one = jnp.sum(grad_aff_one, axis=0)
        grad_pre_one = normalize_back(grad_aff_one * g_one, norm_one, inv_one).astype(jnp.bfloat16)
        dw_one = mm(feat, grad_pre_one, 0, 0)
        dw_one = dw_one + swap(dw_one)
        vecs = jnp.stack([dg_one, db_one, dg_two, db_two])
        vecs = vecs + swap(vecs)
        return loss_val, dw_one, dw_two, dw_three, vecs[0], vecs[1], vecs[2], vecs[3]

    row_spec = P(BATCH_AXIS, None)
    return jax.shard_map(local_step, mesh=mesh, in_specs=(row_spec, row_spec, P(), P(), P(), P(), P(), P(), P(), P()), out_specs=(P(), P(), P(), P(), P(), P(), P(), P()), check_vma=False)
```

time: 888 us -> 410 us (0.46)
  waiting for transfers between devices: 538 us -> 58.2 us
  blocking collectives: 165 us -> 0 us
  matrix products: 76.6 us -> 238 us
  local copies, waits for them, and re-layouts: 66.2 us -> 9.65 us
  other arithmetic: 21.6 us -> 76.7 us
    psum x3 -> x0, waiting for transfers between devices: 538 us -> none  [the longest x1 300 us: local_step(): lax.psum((dw_one, dw_two, dw_three, dg_one, db_one, dg_two, db_two), BATC...]
    psum x5 -> x0, blocking collectives: 165 us -> none  [the longest x3 101 us: global_norm(): lax.psum(jnp.stack([jnp.sum(pre, axis=1), jnp.sum(pre * pre, axis=1)]), B...]
    dot_general x11 -> x10, matrix products: 76.6 us -> 238 us  [mm(): lax.dot_general(a, b, (((ca,), (cb,)), ((), ())), preferred_element_type=...]
    add x0 -> x4, other arithmetic: none -> 41.8 us  [the longest x1 17.7 us: local_step(): dw_two = dw_two + swap(dw_two)]
    all_gather x0 -> x1, waiting for transfers between devices: none -> 39.6 us  [local_step(): both = lax.all_gather(jnp.stack([feat_a, feat_b]), BATCH_AXIS)]
    gather x1 -> x0, local copies, waits for them, and re-layouts: 34 us -> none  [corr_loss(): diag_c = jnp.diagonal(corr)]
    unnamed x49 -> x48, local copies, waits for them, and re-layouts: 32.1 us -> 7.14 us
    convert_element_type x2, other arithmetic: 5.12 us -> 28.2 us  [the longest x1 15.2 us: local_step(): grad_proj = normalize_back(grad_emb, norm_out, inv_out).astype(jnp.bfloat16)]
  transfers between devices with their start and end apart: 3 -> 7, of which waited for: 3 -> 3; matrix products, arithmetic and copies ran while one was open for 7% -> 23% of each run, Pallas kernels for 0% -> 0%
where the time goes in v1:
time: 410 us; the launch traced here: 402 us
  matrix products  238 us (58%)
  other arithmetic  76.7 us (19%)
  waiting for transfers between devices  58.2 us (14%)
  between operations  17.9 us (4%)
  local copies, waits for them, and re-layouts  9.65 us (2%)
    dot_general x10, matrix products, mm(): lax.dot_general(a, b, (((ca,), (cb,)), ((), ())), preferred_element_type=...  238 us
    all_gather x1, waiting for transfers between devices, local_step(): both = lax.all_gather(jnp.stack([feat_a, feat_b]), BATCH_AXIS)  39.6 us
    ppermute x6, waiting for transfers between devices, swap(): return lax.ppermute(value, BATCH_AXIS, pairs)  18.6 us
    add x1, other arithmetic, local_step(): dw_two = dw_two + swap(dw_two)  17.7 us
    add x1, other arithmetic, local_step(): dw_three = dw_three + swap(dw_three)  17.5 us
    convert_element_type x1, other arithmetic, local_step(): grad_proj = normalize_back(grad_emb, norm_out, inv_out).astype(jnp.bfloat16)  15.2 us
    convert_element_type x1, other arithmetic, local_step(): normalize_back(grad_aff_two * g_two, norm_two, inv_two).astype(jnp.bfloat16)  13 us
  transfers between devices with their start and end apart: 7, of which 3 were waited for; matrix products, arithmetic and copies ran while one was open for 23% of the time, Pallas kernels for 0%

profile of v1, /device:TPU:0, one launch (start us, length us, event | category | flops | bytes accessed | tf_op | source)
XLA Modules:
  0.0 402.3 jit_solution(17944128694666573905)
XLA Ops:
  7.2 0.0 all-gather.3.cloned.1.call-start
  7.2 1.8 pad_maximum_fusion
  9.1 0.0 all-gather.3.cloned.1.call-update
  9.1 39.6 %all-gather.3.cloned.1.call-done = bf16[32,128,512]{2,1,0:T(8,128)(2,1)} async-done(((bf16[2,128,512]{2,1,0:T(8,128)(2,1)}), bf16[32,128,512]{2,1,0:T(8,128)(2,1)}) %all-gather.3.cloned.1.call-update) | async-done | bytes 4194320 | tf_op jit(solution)/shard_map/all_gather | solution.py:37
  48.7 1.9 constant_dynamic-slice_fusion
  50.6 1.3 copy-done.4
  51.9 8.6 %fusion.17 = (f32[2048]{0:T(1024)S(1)}, f32[2048]{0:T(1024)S(1)}, f32[2048,2048]{1,0:T(8,128)}) fusion(bf16[2048,512]{1,0:T(8,128)(2,1)S(1)} %bitcast.28, bf16[512,2048]{1,0:T(8,128)(2,1)S(1)} %copy-done), kind=kOutput, calls=%fused_computation.58 | convolution fusion | flops 4307546112 | bytes 20987904 | tf_op jit(solution)/shard_map/dot_general | solution.py:23
  60.7 22.5 %fusion.16 = (f32[2048]{0:T(1024)S(1)}, f32[2048]{0:T(1024)S(1)}, f32[2048,2048]{1,0:T(8,128)}) fusion(bf16[2048,2048]{1,0:T(8,128)(2,1)S(1)} %bitcast.48, f32[2048,2048]{1,0:T(8,128)} %get-tuple-element.34, f32[2048]{0:T(1024)S(1)} %copy-done.12, f32[2048]{0:T(1024)S(1)} %copy-done.14, f32[2048]{0:T(1024)S(1)} %get-tuple-element.33, ...), kind=kOutput, calls=%fused_computation.57 | convolution fusion | flops 17217613824 | bytes 41992192 | tf_op jit(solution)/shard_map/dot_general | solution.py:23
  83.2 20.8 %fusion.15 = (f32[2048]{0:T(1024)S(1)}, f32[2048]{0:T(1024)S(1)}, f32[2048,2048]{1,0:T(8,128)S(1)}) fusion(bf16[2048,2048]{1,0:T(8,128)(2,1)S(1)} %bitcast.46, f32[2048,2048]{1,0:T(8,128)} %get-tuple-element.35, f32[2048]{0:T(1024)S(1)} %copy-done.11, f32[2048]{0:T(1024)S(1)} %copy-done.6, f32[2048]{0:T(1024)S(1)} %get-tuple-element.31, ...), kind=kOutput, calls=%fused_computation.56 | convolution fusion | flops 17217613824 | bytes 41992192 | tf_op jit(solution)/shard_map/dot_general | solution.py:23
  104.1 5.7 %copy-done.2 = f32[2048,2048]{1,0:T(8,128)} copy-done((f32[2048,2048]{1,0:T(8,128)}, f32[2048,2048]{1,0:T(8,128)S(1)}, u32[]{:S(2)}) %copy-start.2) | copy-done | bytes 16777240
  109.8 4.8 %fusion = bf16[2048,2048]{1,0:T(8,128)(2,1)} fusion(f32[2048,2048]{1,0:T(8,128)S(1)} %get-tuple-element.36, f32[2048]{0:T(1024)S(1)} %get-tuple-element.29, f32[2048]{0:T(1024)S(1)} %get-tuple-element.28), kind=kLoop, calls=%fused_computation.26 | loop fusion | flops 12582912 | bytes 25182208 | tf_op jit(solution)/shard_map/convert_element_type | solution.py:46
  114.6 0.2 collective-permute-start
  115.5 12.2 %collective-permute-done = bf16[2048,2048]{1,0:T(8,128)(2,1)} collective-permute-done((bf16[2048,2048]{1,0:T(8,128)(2,1)}, bf16[2048,2048]{1,0:T(8,128)(2,1)}, u32[]{:S(2)}, u32[]{:S(2)}) %collective-permute-start) | collective-permute-done | bytes 8388640 | tf_op jit(solution)/shard_map/ppermute | solution.py:31
  127.7 30.7 %select_reduce_fusion = (f32[]{:T(128)}, f32[2048,2048]{1,0:T(8,128)}) fusion(f32[]{:T(128)S(6)} %mul.180, bf16[2048,2048]{1,0:T(8,128)(2,1)} %fusion, bf16[2048,2048]{1,0:T(8,128)(2,1)} %collective-permute-done), kind=kOutput, calls=%fused_computation.9 | convolution fusion | flops 17213423616 | bytes 33554440 | tf_op jit(solution)/shard_map/dot_general | solution.py:23
  158.4 28.4 %multiply_reduce_fusion.10 = (f32[2048]{0:T(1024)S(1)}, f32[2048]{0:T(1024)S(1)}, f32[2048,2048]{1,0:T(8,128)}) fusion(f32[2048]{0:T(1024)S(1)} %get-tuple-element.29, f32[2048,2048]{1,0:T(8,128)} %copy-done.2, f32[2048]{0:T(1024)S(1)} %get-tuple-element.28, bf16[2048,2048]{1,0:T(8,128)(2,1)} %collective-permute-done, f32[2048,2048]{1,0:T(8,128)} %get-tuple-element.38, ...), kind=kOutput, calls=%fused_computation.25 | convolution fusion | flops 17234391040 | bytes 58753028 | tf_op jit(solution)/shard_map/dot_general | solution.py:23
  186.9 15.2 %multiply_convert_fusion.2 = bf16[2048,2048]{1,0:T(8,128)(2,1)} fusion(f32[2048,2048]{1,0:T(8,128)} %get-tuple-element.39, f32[2048,2048]{1,0:T(8,128)} %copy-done.2, f32[2048]{0:T(1024)S(1)} %get-tuple-element.42, f32[2048]{0:T(1024)S(1)} %get-tuple-element.43, f32[2048]{0:T(1024)S(1)} %get-tuple-element.29, f32[2048]{0:T(1024)S(1)} %get-tuple-element.28), kind=kLoop, calls=%fused_computation.6 | loop fusion | flops 33554432 | bytes 41975808 | tf_op jit(solution)/shard_map/convert_element_type | solution.py:54
  202.0 31.6 %multiply_reduce_fusion = (f32[2048]{0:T(1024)S(1)}, f32[2048]{0:T(1024)S(1)}, f32[2048]{0:T(1024)S(1)}, f32[2048]{0:T(1024)S(1)}, f32[2048,2048]{1,0:T(8,128)}) fusion(f32[2048,2048]{1,0:T(8,128)} %get-tuple-element.35, f32[2048]{0:T(1024)S(1)} %get-tuple-element.31, f32[2048]{0:T(1024)S(1)} %get-tuple-element.30, f32[2048]{0:T(1024)S(1)} %copy-done.6, ...), kind=kOutput, calls=%fused_computation | convolution fusion | flops 17234386944 | bytes 50397184 | tf_op jit(solution)/shard_map/dot_general | solution.py:23
  233.7 13.0 %multiply_convert_fusion.1 = bf16[2048,2048]{1,0:T(8,128)(2,1)S(1)} fusion(f32[2048,2048]{1,0:T(8,128)} %get-tuple-element.40, f32[2048,2048]{1,0:T(8,128)} %get-tuple-element.35, f32[2048]{0:T(1024)S(1)} %broadcast_multiply_fusion.2, f32[2048]{0:T(1024)S(1)} %broadcast_multiply_fusion.3, f32[2048]{0:T(1024)S(1)} %copy-done.6, ...), kind=kLoop, calls=%fused_computation.4 | loop fusion | flops 33554432 | bytes 41984000 | tf_op jit(solution)/shard_map/convert_element_type | solution.py:60
  246.7 26.0 %fusion.11 = f32[2048,2048]{1,0:T(8,128)} fusion(bf16[2048,2048]{1,0:T(8,128)(2,1)S(1)} %multiply_convert_fusion.1, f32[2048,2048]{1,0:T(8,128)} %get-tuple-element.34, f32[2048]{0:T(1024)S(1)} %copy-done.13, f32[2048]{0:T(1024)S(1)} %copy-done.15, f32[2048]{0:T(1024)S(1)} %copy-done.10, f32[2048]{0:T(1024)S(1)} %copy-done.8), kind=kOutput, calls=%fused_computation.52 | convolution fusion | flops 17205035008 | bytes 41975808 | tf_op jit(solution)/shard_map/dot_general | solution.py:23
  272.7 0.3 collective-permute-start.3
  273.0 22.5 %fusion.13 = f32[2048,2048]{1,0:T(8,128)} fusion(bf16[2048,2048]{1,0:T(8,128)(2,1)} %multiply_convert_fusion.2, f32[2048,2048]{1,0:T(8,128)S(1)} %bitcast.27, f32[2048]{0:T(1024)S(1)} %copy-done.11, f32[2048]{0:T(1024)S(1)} %copy-done.6, f32[2048]{0:T(1024)S(1)} %get-tuple-element.31, f32[2048]{0:T(1024)S(1)} %get-tuple-element.30), kind=kOutput, calls=%fused_computation.54 | convolution fusion | flops 17205035008 | bytes 41975808 | tf_op jit(solution)/shard_map/dot_general | solution.py:23
  295.5 0.2 collective-permute-start.4
  295.7 31.6 %multiply_reduce_fusion.1 = (f32[2048]{0:T(1024)S(1)}, f32[2048]{0:T(1024)S(1)}, f32[2048]{0:T(1024)S(1)}, f32[2048]{0:T(1024)S(1)}, f32[2048,2048]{1,0:T(8,128)}) fusion(f32[2048,2048]{1,0:T(8,128)} %get-tuple-element.34, f32[2048]{0:T(1024)S(1)} %copy-done.10, f32[2048]{0:T(1024)S(1)} %copy-done.8, f32[2048]{0:T(1024)S(1)} %copy-done.15, ...), kind=kOutput, calls=%fused_computation.1 | convolution fusion | flops 17234386944 | bytes 50397184 | tf_op jit(solution)/shard_map/dot_general | solution.py:23
  327.3 15.5 %fusion.6 = f32[512,2048]{1,0:T(8,128)} fusion(bf16[2048,512]{1,0:T(8,128)(2,1)S(1)} %bitcast.29, f32[2048,2048]{1,0:T(8,128)} %get-tuple-element.41, f32[2048,2048]{1,0:T(8,128)} %get-tuple-element.34, f32[2048]{0:T(1024)S(1)} %broadcast_multiply_fusion, f32[2048]{0:T(1024)S(1)} %broadcast_multiply_fusion.1, f32[2048]{0:T(1024)S(1)} %copy-done.15, ...), kind=kOutput, calls=%fused_computation.32 | convolution fusion | flops 4328521728 | bytes 39886848 | tf_op jit(solution)/shard_map/dot_general | solution.py:23
  342.8 0.3 collective-permute-start.2
  343.1 0.3 collective-permute-start.5
  343.4 0.3 collective-permute-start.1
  343.7 6.3 %collective-permute-done.1 = f32[]{:T(128)} collective-permute-done((f32[]{:T(128)}, f32[]{:T(128)}, u32[]{:S(2)}, u32[]{:S(2)}) %collective-permute-start.1) | collective-permute-done | bytes 36 | tf_op jit(solution)/shard_map/ppermute | solution.py:31
  351.4 0.6 fusion.18
  352.0 6.6 %add.66 = f32[512,2048]{1,0:T(8,128)} add(f32[512,2048]{1,0:T(8,128)} %fusion.6, f32[512,2048]{1,0:T(8,128)} %collective-permute-done.2) | non-fusion elementwise | flops 1048576 | bytes 12582912 | tf_op jit(solution)/shard_map/add | solution.py:68
  358.6 17.7 %add.67 = f32[2048,2048]{1,0:T(8,128)} add(f32[2048,2048]{1,0:T(8,128)} %fusion.11, f32[2048,2048]{1,0:T(8,128)} %collective-permute-done.3) | non-fusion elementwise | flops 4194304 | bytes 50331648 | tf_op jit(solution)/shard_map/add | solution.py:62
  376.3 17.5 %add.68 = f32[2048,2048]{1,0:T(8,128)} add(f32[2048,2048]{1,0:T(8,128)} %fusion.13, f32[2048,2048]{1,0:T(8,128)} %collective-permute-done.4) | non-fusion elementwise | flops 4194304 | bytes 50331648 | tf_op jit(solution)/shard_map/add | solution.py:56
  (63 shorter events, 0.3 us)
Async XLA Ops:
  7.2 44.7 %copy-start = (bf16[512,2048]{1,0:T(8,128)(2,1)S(1)}, bf16[512,2048]{1,0:T(8,128)(2,1)}, u32[]{:S(2)}) copy-start(bf16[512,2048]{1,0:T(8,128)(2,1)} %param.12) | copy-start | bytes 6291460
  7.2 41.5 %all-gather.3.cloned.1.call-start = ((), (), s32[]{:S(2)}) async-start(), calls=%async_computation | async-start | bytes 4456448 | tf_op jit(solution)/shard_map/all_gather | solution.py:37
  48.7 11.9 %slice-start.6 = ((s8[8388608]{0:T(1024)(128)(4,1)}), s8[4194304]{0:T(1024)(128)(4,1)S(1)}, s32[]{:S(2)}) async-start(s8[8388608]{0:T(1024)(128)(4,1)} %bitcast.47), calls=%async_computation.7 | async-start | bytes 8388608
  48.7 11.9 %copy-start.12 = (f32[2048]{0:T(1024)S(1)}, f32[2048]{0:T(1024)}, u32[]{:S(2)}) copy-start(f32[2048]{0:T(1024)} %param.16) | copy-start | bytes 24580
  48.7 11.9 %copy-start.14 = (f32[2048]{0:T(1024)S(1)}, f32[2048]{0:T(1024)}, u32[]{:S(2)}) copy-start(f32[2048]{0:T(1024)} %param.15) | copy-start | bytes 24580
  50.6 1.3 copy-start.4
  51.9 8.7 %slice-start.7 = ((s8[8388608]{0:T(1024)(128)(4,1)}), s8[4194304]{0:T(1024)(128)(4,1)S(1)}, s32[]{:S(2)}) async-start(s8[8388608]{0:T(1024)(128)(4,1)} %bitcast.47), calls=%async_computation.8 | async-start | bytes 8388608
  51.9 31.3 %slice-start.4 = ((s8[8388608]{0:T(1024)(128)(4,1)}), s8[4194304]{0:T(1024)(128)(4,1)S(1)}, s32[]{:S(2)}) async-start(s8[8388608]{0:T(1024)(128)(4,1)} %bitcast.45), calls=%async_computation.5 | async-start | bytes 8388608
  60.6 22.6 %copy-start.7 = (f32[2048]{0:T(1024)}, f32[2048]{0:T(1024)S(1)}, u32[]{:S(2)}) copy-start(f32[2048]{0:T(1024)S(1)} %get-tuple-element.32) | copy-start | bytes 24580
  60.6 22.6 %copy-start.9 = (f32[2048]{0:T(1024)}, f32[2048]{0:T(1024)S(1)}, u32[]{:S(2)}) copy-start(f32[2048]{0:T(1024)S(1)} %get-tuple-element.33) | copy-start | bytes 24580
  60.6 22.6 %copy-start.6 = (f32[2048]{0:T(1024)S(1)}, f32[2048]{0:T(1024)}, u32[]{:S(2)}) copy-start(f32[2048]{0:T(1024)} %param.17) | copy-start | bytes 24580
  60.6 22.6 %slice-start.5 = ((s8[8388608]{0:T(1024)(128)(4,1)}), s8[4194304]{0:T(1024)(128)(4,1)S(1)}, s32[]{:S(2)}) async-start(s8[8388608]{0:T(1024)(128)(4,1)} %bitcast.45), calls=%async_computation.6 | async-start | bytes 8388608
  60.6 22.6 %copy-start.11 = (f32[2048]{0:T(1024)S(1)}, f32[2048]{0:T(1024)}, u32[]{:S(2)}) copy-start(f32[2048]{0:T(1024)} %param.18) | copy-start | bytes 24580
  104.1 5.7 %copy-start.2 = (f32[2048,2048]{1,0:T(8,128)}, f32[2048,2048]{1,0:T(8,128)S(1)}, u32[]{:S(2)}) copy-start(f32[2048,2048]{1,0:T(8,128)S(1)} %get-tuple-element.36) | copy-start | bytes 50331652
  114.6 13.1 %collective-permute-start = (bf16[2048,2048]{1,0:T(8,128)(2,1)}, bf16[2048,2048]{1,0:T(8,128)(2,1)}, u32[]{:S(2)}, u32[]{:S(2)}) collective-permute-start(bf16[2048,2048]{1,0:T(8,128)(2,1)} %fusion), channel_id=1, source_target_pairs={{0,1},{1,0},{2,3},{3,2},{4,5},{5,4},{6,7},{7,6},{8,9},{9,8},{10,11... | collective-permute-start | bytes 25165832 | tf_op jit(solution)/shard_map/ppermute | solution.py:31
  233.6 13.1 %copy-start.8 = (f32[2048]{0:T(1024)S(1)}, f32[2048]{0:T(1024)}, u32[]{:S(2)}) copy-start(f32[2048]{0:T(1024)} %copy-done.7) | copy-start | bytes 24580
  233.6 13.1 %copy-start.10 = (f32[2048]{0:T(1024)S(1)}, f32[2048]{0:T(1024)}, u32[]{:S(2)}) copy-start(f32[2048]{0:T(1024)} %copy-done.9) | copy-start | bytes 24580
  233.6 13.1 %copy-start.13 = (f32[2048]{0:T(1024)S(1)}, f32[2048]{0:T(1024)}, u32[]{:S(2)}) copy-start(f32[2048]{0:T(1024)} %param.16) | copy-start | bytes 24580
  233.6 13.1 %copy-start.15 = (f32[2048]{0:T(1024)S(1)}, f32[2048]{0:T(1024)}, u32[]{:S(2)}) copy-start(f32[2048]{0:T(1024)} %param.15) | copy-start | bytes 24580
  233.7 39.3 %slice-start = ((s8[16777216]{0:T(1024)(128)(4,1)}), s8[4194304]{0:T(1024)(128)(4,1)S(1)}, s32[]{:S(2)}) async-start(s8[16777216]{0:T(1024)(128)(4,1)} %bitcast.26), calls=%async_computation.1 | async-start | bytes 8388608
  233.7 39.3 %slice-start.1 = ((s8[16777216]{0:T(1024)(128)(4,1)}), s8[4194304]{0:T(1024)(128)(4,1)S(1)}, s32[]{:S(2)}) async-start(s8[16777216]{0:T(1024)(128)(4,1)} %bitcast.26), calls=%async_computation.2 | async-start | bytes 8388608
  246.7 26.0 %copy-start.3 = (bf16[2048,2048]{1,0:T(8,128)(2,1)}, bf16[2048,2048]{1,0:T(8,128)(2,1)S(1)}, u32[]{:S(2)}) copy-start(bf16[2048,2048]{1,0:T(8,128)(2,1)S(1)} %multiply_convert_fusion.1) | copy-start | bytes 25165828
  246.7 26.3 %slice-start.2 = ((s8[16777216]{0:T(1024)(128)(4,1)}), s8[4194304]{0:T(1024)(128)(4,1)S(1)}, s32[]{:S(2)}) async-start(s8[16777216]{0:T(1024)(128)(4,1)} %bitcast.26), calls=%async_computation.3 | async-start | bytes 8388608
  246.7 26.3 %slice-start.3 = ((s8[16777216]{0:T(1024)(128)(4,1)}), s8[4194304]{0:T(1024)(128)(4,1)S(1)}, s32[]{:S(2)}) async-start(s8[16777216]{0:T(1024)(128)(4,1)} %bitcast.26), calls=%async_computation.4 | async-start | bytes 8388608
  272.7 85.9 %collective-permute-start.3 = (f32[2048,2048]{1,0:T(8,128)}, f32[2048,2048]{1,0:T(8,128)}, u32[]{:S(2)}, u32[]{:S(2)}) collective-permute-start(f32[2048,2048]{1,0:T(8,128)} %fusion.11), channel_id=1, source_target_pairs={{0,1},{1,0},{2,3},{3,2},{4,5},{5,4},{6,7},{7,6},{8,9},{9,8},{10,11... | collective-permute-start | bytes 50331656 | tf_op jit(solution)/shard_map/ppermute | solution.py:31
  295.5 31.8 %copy-start.5 = (bf16[16,1,128,512]{3,2,1,0:T(8,128)(2,1)S(1)}, bf16[16,1,128,512]{3,2,1,0:T(8,128)(2,1)}, u32[]{:S(2)}) copy-start(bf16[16,1,128,512]{3,2,1,0:T(8,128)(2,1)} %copy-done.4) | copy-start | bytes 6291460
  295.5 80.8 %collective-permute-start.4 = (f32[2048,2048]{1,0:T(8,128)}, f32[2048,2048]{1,0:T(8,128)}, u32[]{:S(2)}, u32[]{:S(2)}) collective-permute-start(f32[2048,2048]{1,0:T(8,128)} %fusion.13), channel_id=1, source_target_pairs={{0,1},{1,0},{2,3},{3,2},{4,5},{5,4},{6,7},{7,6},{8,9},{9,8},{10,11... | collective-permute-start | bytes 50331656 | tf_op jit(solution)/shard_map/ppermute | solution.py:31
  342.8 9.2 %collective-permute-start.2 = (f32[512,2048]{1,0:T(8,128)}, f32[512,2048]{1,0:T(8,128)}, u32[]{:S(2)}, u32[]{:S(2)}) collective-permute-start(f32[512,2048]{1,0:T(8,128)} %fusion.6), channel_id=1, source_target_pairs={{0,1},{1,0},{2,3},{3,2},{4,5},{5,4},{6,7},{7,6},{8,9},{9,8},{10,11... | collective-permute-start | bytes 12582920 | tf_op jit(solution)/shard_map/ppermute | solution.py:31
  343.1 8.2 %collective-permute-start.5 = (f32[4,2048]{1,0:T(4,128)S(1)}, f32[4,2048]{1,0:T(4,128)S(1)}, u32[]{:S(2)}, u32[]{:S(2)}) collective-permute-start(f32[4,2048]{1,0:T(4,128)S(1)} %pad_maximum_fusion.1), channel_id=1, source_target_pairs={{0,1},{1,0},{2,3},{3,2},{4,5},{5,4},{6,7},{7,6},{8,9},{9,8},{10,11... | collective-permute-start | bytes 98312 | tf_op jit(solution)/shard_map/ppermute | solution.py:31
  343.4 6.6 %collective-permute-start.1 = (f32[]{:T(128)}, f32[]{:T(128)}, u32[]{:S(2)}, u32[]{:S(2)}) collective-permute-start(f32[]{:T(128)} %get-tuple-element.37), channel_id=1, source_target_pairs={{0,1},{1,0},{2,3},{3,2},{4,5},{5,4},{6,7},{7,6},{8,9},{9,8},{10,11... | collective-permute-start | bytes 20 | tf_op jit(solution)/shard_map/ppermute | solution.py:31
  358.6 35.2 %copy-start.1 = (bf16[512,2048]{1,0:T(8,128)(2,1)S(1)}, bf16[512,2048]{1,0:T(8,128)(2,1)}, u32[]{:S(2)}) copy-start(bf16[512,2048]{1,0:T(8,128)(2,1)} %param.12) | copy-start | bytes 6291460
Sparse Core Ops, SparseCore 0:
  10.8 37.8 all-gather.2
